TPU v7x, 32 devices: a whole 2x2x4 slice. The times are simulated.
32 devices in a mesh: tm: 8 (over z, y), node: 4 (over x, core).
Axes of the slice: x: 2, y: 2, z: 4, core: 2. Of those that a mesh axis runs over, the one named last changes fastest.
Arguments:
- slice_starts: float32 [8, 32, 16384], P('tm'), may hold values from -1 to 1
- coupling: float32 [32, 16384], replicated, may hold values from 0.03 to 0.25
Outputs:
- node_values: float32 [8, 4, 32, 16384], P('tm', 'node')
- residual_log: float32 [3, 32], replicated
All inputs are finite; a program needn't handle non-finite values.
Results may differ from a plain program's by a relative error of at most 0.0001.
Values sent between devices are 32-bit elements.
A program may use at most 128 MiB of HBM per device.

v0:
```python
import functools
import jax
import jax.numpy as jnp
from jax import lax
from jax.experimental import pallas as pl
from jax.experimental.pallas import tpu as pltpu
from jax.sharding import PartitionSpec as P

M = 4
CHUNKS = 8
STEP = 8
LANE = 128
HALO = 3
PAD = 4
MESH = pl.DeviceIdType.MESH

time_step = 0.5
log_floor = 0.05


def legendre_gap(point, node_count):
    before = 1.0
    current = point
    for degree in range(1, node_count):
        following = ((2 * degree + 1) * point * current - degree * before) / (degree + 1)
        before = current
        current = following
    return current - before


def collocation(node_count):
    points = []
    samples = 4000
    for sample_index in range(samples - 1):
        lower_end = -1.0 + 2.0 * sample_index / samples
        upper_end = -1.0 + 2.0 * (sample_index + 1) / samples
        lower_value = legendre_gap(lower_end, node_count)
        upper_value = legendre_gap(upper_end, node_count)
        if lower_value * upper_value < 0.0:
            for halving in range(80):
                middle = 0.5 * (lower_end + upper_end)
                middle_value = legendre_gap(middle, node_count)
                if lower_value * middle_value <= 0.0:
                    upper_end = middle
                else:
                    lower_end = middle
                    lower_value = middle_value
            points.append(0.5 * (lower_end + upper_end))
    points.append(1.0)
    node_times = [(point + 1.0) / 2.0 for point in points]
    matrix = [[0.0] * node_count for row_index in range(node_count)]
    for column in range(node_count):
        coeffs = [1.0]
        for other in range(node_count):
            if other != column:
                scale = node_times[column] - node_times[other]
                shifted = [0.0] + coeffs
                scaled = [value * node_times[other] for value in coeffs] + [0.0]
                coeffs = [(shifted[power] - scaled[power]) / scale for power in range(len(shifted))]
        for row_index in range(node_count):
            upper_time = node_times[row_index]
            matrix[row_index][column] = sum(
                (
                    coeffs[power] * upper_time ** (power + 1) / (power + 1)
                    for power in range(len(coeffs))
                )
            )
    return (node_times, matrix)


def kernel(
    slices, rows, cells,
    start_hbm, coupling_hbm, out_hbm, log_ref,
    own, couple, prev1, prev2, prev3, here, there, mid, before, result,
    acc, part_tm, part_node,
    load_sem, s_prev1, r_prev1, s_prev2, r_prev2, s_prev3, r_prev3,
    s_out, r_out, local_sem, s_tm, r_tm, s_node, r_node,
):
    p = lax.axis_index("tm")
    n = lax.axis_index("node")
    chunk = cells // CHUNKS
    tiles = chunk // LANE
    all_tiles = cells // LANE
    my_rows = pl.ds(pl.multiple_of(n * rows, rows), rows)
    node_times, matrix = collocation(M)
    weight = [[time_step * value for value in line] for line in matrix]
    total = [sum(line) for line in weight]
    implicit = [time_step * moment / M for moment in node_times]
    even = lax.rem(p, 2) == 0
    first = p == 0
    second = p == 1

    loads = []
    for index, (source, target) in enumerate(
        ((start_hbm.at[0, my_rows], own), (coupling_hbm.at[my_rows], couple))
    ):
        for piece, (lo, to, size) in enumerate(
            ((0, PAD * LANE, cells), (cells - HALO * LANE, LANE, HALO * LANE), (0, PAD * LANE + cells, HALO * LANE))
        ):
            copy = pltpu.make_async_copy(
                source.at[:, pl.ds(lo, size)],
                target.at[:, pl.ds(to, size)],
                load_sem.at[index, piece],
            )
            copy.start()
            loads.append(copy)

    barrier = pltpu.get_barrier_semaphore()
    for step in range(1, slices):
        pl.semaphore_signal(
            barrier, inc=1, device_id={"tm": lax.rem(p + step, slices), "node": n}, device_id_type=MESH
        )
    for step in range(1, M):
        pl.semaphore_signal(
            barrier, inc=1, device_id={"tm": p, "node": lax.rem(n + step, M)}, device_id_type=MESH
        )
    pl.semaphore_wait(barrier, slices - 1 + M - 1)
    for copy in loads:
        copy.wait()

    def remote(source, target, send, recv, tm, node):
        return pltpu.make_async_remote_copy(
            src_ref=source, dst_ref=target, send_sem=send, recv_sem=recv,
            device_id={"tm": tm, "node": node}, device_id_type=MESH,
        )

    partner = jnp.where(even, p + 1, p - 1)
    ahead = lax.rem(p + 2, slices)

    def part(ref, c):
        begin = (c * tiles + HALO if c else -HALO) + PAD
        end = (c + 1) * tiles + HALO + PAD
        return ref.at[:, pl.ds(begin * LANE, (end - begin) * LANE)]

    def to_partner_own(c):
        return remote(part(own, c), part(prev1, c), s_prev1.at[c], r_prev1.at[c], partner, n)

    def to_partner_forward(c):
        return remote(part(prev2, c), part(prev1, c), s_prev1.at[c], r_prev1.at[c], partner, n)

    def ahead_own(c):
        return remote(part(own, c), part(prev2, c), s_prev2.at[c], r_prev2.at[c], ahead, n)

    def ahead_forward(c):
        return remote(part(prev1, c), part(prev3, c), s_prev3.at[c], r_prev3.at[c], ahead, n)

    has_behind = p >= 2
    has_ahead = p + 2 < slices
    odd = jnp.logical_not(even)

    def start_ahead(c):
        @pl.when(has_ahead)
        def _():
            ahead_own(c).start()

    @pl.when(even)
    def _():
        for c in range(CHUNKS):
            to_partner_own(c).start()
    def pass_across(c):
        @pl.when(has_behind)
        def _():
            ahead_own(c).wait_recv()

        @pl.when(jnp.logical_and(odd, has_behind))
        def _():
            to_partner_forward(c).start()

    def pass_ahead(c):
        @pl.when(odd)
        def _():
            to_partner_own(c).wait_recv()

        @pl.when(jnp.logical_and(even, has_behind))
        def _():
            to_partner_forward(c).wait_recv()

        @pl.when(jnp.logical_and(has_ahead, jnp.logical_not(first)))
        def _():
            ahead_forward(c).start()

    for c in range(3):
        start_ahead(c)

    acc[...] = jnp.zeros_like(acc)

    def diffusion(v, c, k):
        size = (k + 2) * LANE
        right = pltpu.roll(v, size - 1, 1)
        flux = c * (right - v)
        left = pltpu.roll(flux, 1, 1)
        return (flux - left)[:, LANE:LANE + k * LANE]

    def two_steps(base, u, square, reaction, a):
        s = (3.0 * a) * square - a
        d = 1.0 + s
        top = base + u * s
        target = base - a * reaction
        dd = d * d
        tt = top * top
        above = target * (d * dd) + (2.0 * a) * (top * tt)
        below = d * ((1.0 - a) * dd + (3.0 * a) * tt)
        guess = pl.reciprocal(below, approx=True)
        return above * (guess * (2.0 - below * guess))

    def folded(value, k):
        out = value[:, :LANE]
        for piece in range(1, k):
            out = out + value[:, piece * LANE:(piece + 1) * LANE]
        return out

    def run(begin, end, block, counted):
        count = (end - begin) // STEP

        def step(i, carry):
            block(begin + i * STEP, STEP, counted)
            return carry

        lax.fori_loop(0, count, step, 0)
        if begin + count * STEP < end:
            block(begin + count * STEP, end - begin - count * STEP, counted)

    def over(c, lag, block):
        begin = c * tiles + lag if c else 0
        end = min((c + 1) * tiles + lag, all_tiles)
        if c == 0 and lag:
            block(-lag, lag, False)
        run(begin, end, block, True)
        if c == CHUNKS - 1 and lag:
            block(all_tiles, lag, False)

    def lanes(offset):
        return offset * LANE if isinstance(offset, int) else pl.multiple_of(offset * LANE, LANE)

    def wide(tile, k):
        return pl.ds(lanes(tile + PAD - 1), (k + 2) * LANE)

    def centre(tile, k):
        return pl.ds(lanes(tile + PAD), k * LANE)

    pass_across(0)
    pass_across(1)
    pass_ahead(0)
    for c in range(CHUNKS):
        base_lane = c * chunk

        if c + 3 < CHUNKS:
            start_ahead(c + 3)
        if c + 1 < CHUNKS:
            pass_ahead(c + 1)

        @pl.when(p >= 3)
        def _():
            ahead_forward(c).wait_recv()

        def stage_a(tile, k, counted):
            mid_slice = slice(LANE, LANE + k * LANE)
            cw = couple[:, wide(tile, k)]
            at = centre(tile, k)
            vw = own[:, wide(tile, k)]
            v = vw[:, mid_slice]
            p1w = jnp.where(first, vw, prev1[:, wide(tile, k)])
            p1 = p1w[:, mid_slice]
            p2w = jnp.where(p <= 1, p1w, prev2[:, wide(tile, k)])
            p2 = p2w[:, mid_slice]
            p3 = jnp.where(p <= 2, p2, prev3[:, at])

            square = v * v
            reaction = v - v * square
            forcing = diffusion(vw, cw, k) + reaction
            found = None
            for m in range(M):
                base = p1 + total[m] * forcing
                if counted:
                    defect = base - v
                    found = defect * defect if found is None else found + defect * defect
                here[m, :, at] = two_steps(base, v, square, reaction, implicit[m])
            if counted:
                acc[0] += folded(found, k)

            square = p1 * p1
            reaction = p1 - p1 * square
            forcing = diffusion(p1w, cw, k) + reaction
            for m in range(M):
                there[m, :, at] = two_steps(p2 + total[m] * forcing, p1, square, reaction, implicit[m])

            square = p2 * p2
            reaction = p2 - p2 * square
            forcing = diffusion(p2w, cw, k) + reaction
            last = two_steps(
                p3 + total[M - 1] * forcing, p2, square, reaction, implicit[M - 1]
            )
            before[:, at] = jnp.where(second, p1, last)

        over(c, 2, stage_a)
        if c + 2 < CHUNKS:
            pass_across(c + 2)

        def update(source, begin, cw, tile, k, which, counted):
            values = []
            forcings = []
            for m in range(M):
                vw = source[m, :, wide(tile, k)]
                v = vw[:, LANE:LANE + k * LANE]
                square = v * v
                reaction = v - v * square
                values.append((v, square, reaction))
                forcings.append(diffusion(vw, cw, k) + reaction)
            found = None
            outputs = []
            for m in range(M):
                base = begin
                for j in range(M):
                    base = base + weight[m][j] * forcings[j]
                v, square, reaction = values[m]
                if counted:
                    defect = base - v
                    found = defect * defect if found is None else found + defect * defect
                outputs.append(two_steps(base, v, square, reaction, implicit[m]))
            if counted:
                acc[which] += folded(found, k)
            return outputs

        def stage_b(tile, k, counted):
            cw = couple[:, wide(tile, k)]
            at = centre(tile, k)
            begin = jnp.where(first, own[:, centre(tile, k)], there[M - 1, :, at])
            outputs = update(here, begin, cw, tile, k, 1, counted)
            for m in range(M):
                mid[m, :, at] = outputs[m]
            mixed = None
            mixed_reaction = None
            for m in range(M):
                w = weight[M - 1][m]
                vw = there[m, :, wide(tile, k)]
                v = vw[:, LANE:LANE + k * LANE]
                square = v * v
                reaction = v - v * square
                mixed = w * vw if mixed is None else mixed + w * vw
                mixed_reaction = w * reaction if mixed_reaction is None else mixed_reaction + w * reaction
            base = before[:, at] + (diffusion(mixed, cw, k) + mixed_reaction)
            last = two_steps(base, v, square, reaction, implicit[M - 1])
            before[:, at] = jnp.where(first, own[:, centre(tile, k)], last)

        over(c, 1, stage_b)

        def stage_c(tile, k, counted):
            cw = couple[:, wide(tile, k)]
            outputs = update(mid, before[:, centre(tile, k)], cw, tile, k, 2, counted)
            at = pl.ds(lanes(tile - c * tiles), k * LANE)
            for m in range(M):
                result[c, m, :, at] = outputs[m]

        over(c, 0, stage_c)

        target = out_hbm.at[my_rows, pl.ds(base_lane, chunk)]
        for step in (2, 3, 1):
            peer = lax.rem(n + step, M)
            remote(result.at[c, peer], target, s_out.at[c, step], r_out.at[c, step], p, peer).start()
        pltpu.make_async_copy(result.at[c, n], target, local_sem.at[c]).start()

    lane = lax.broadcasted_iota(jnp.int32, (rows, LANE), 1)
    sub = lax.broadcasted_iota(jnp.int32, (rows, LANE), 0)
    place = lax.broadcasted_iota(jnp.int32, (8, LANE), 0)
    tile_value = jnp.zeros((8, LANE), jnp.float32)
    for which in range(3):
        per_system = jnp.sum(acc[which], axis=1, keepdims=True)
        row = jnp.sum(
            jnp.where(lane == n * rows + sub, per_system, 0.0), axis=0, keepdims=True
        )
        tile_value = tile_value + jnp.where(place == which, row, 0.0)
    part_tm[p] = tile_value
    sends = []
    for step in range(1, slices):
        copy = remote(
            part_tm.at[p], part_tm.at[p], s_tm.at[step], r_tm.at[step], lax.rem(p + step, slices), n
        )
        copy.start()
        sends.append(copy)
    for step in range(1, slices):
        source = lax.rem(p - step + slices, slices)
        remote(part_tm.at[source], part_tm.at[source], s_tm.at[step], r_tm.at[step], p, n).wait_recv()
    summed = part_tm[0]
    for index in range(1, slices):
        summed = summed + part_tm[index]
    part_node[n] = summed
    for step in range(1, M):
        copy = remote(
            part_node.at[n], part_node.at[n], s_node.at[step], r_node.at[step], p, lax.rem(n + step, M)
        )
        copy.start()
        sends.append(copy)
    for step in range(1, M):
        source = lax.rem(n - step + M, M)
        remote(part_node.at[source], part_node.at[source], s_node.at[step], r_node.at[step], p, n).wait_recv()
    summed = part_node[0]
    for index in range(1, M):
        summed = summed + part_node[index]
    log_ref[...] = jnp.log(log_floor + summed / (slices * M * cells))

    for copy in sends:
        copy.wait_send()
    for c in range(CHUNKS):
        here_rows = pl.ds(c * chunk, chunk)
        for step in range(1, M):
            source = lax.rem(n - step + M, M)
            landed = out_hbm.at[pl.ds(pl.multiple_of(source * rows, rows), rows), here_rows]
            arrived = remote(result.at[c, n], landed, s_out.at[c, step], r_out.at[c, step], p, n)
            arrived.wait_recv()
            arrived.wait_send()
        pltpu.make_async_copy(result.at[c, n], out_hbm.at[my_rows, here_rows], local_sem.at[c]).wait()

        @pl.when(has_ahead)
        def _():
            ahead_own(c).wait_send()

        @pl.when(jnp.logical_and(has_ahead, jnp.logical_not(first)))
        def _():
            ahead_forward(c).wait_send()

        @pl.when(even)
        def _():
            to_partner_own(c).wait_send()

        @pl.when(jnp.logical_and(odd, has_behind))
        def _():
            to_partner_forward(c).wait_send()


def solution(mesh):
    slices = mesh.shape["tm"]

    def body(slice_starts, coupling):
        systems, cells = coupling.shape
        rows = systems // M
        chunk = cells // CHUNKS
        padded = cells + 2 * PAD * LANE
        f32 = jnp.float32
        dma = pltpu.SemaphoreType.DMA
        anywhere = pl.BlockSpec(memory_space=pl.ANY)
        values, logs = pl.pallas_call(
            functools.partial(kernel, slices, rows, cells),
            out_shape=(
                jax.ShapeDtypeStruct((systems, cells), f32),
                jax.ShapeDtypeStruct((8, LANE), f32),
            ),
            in_specs=[anywhere, anywhere],
            out_specs=(anywhere, pl.BlockSpec(memory_space=pltpu.VMEM)),
            scratch_shapes=[
                pltpu.VMEM((rows, padded), f32),
                pltpu.VMEM((rows, padded), f32),
                pltpu.VMEM((rows, padded), f32),
                pltpu.VMEM((rows, padded), f32),
                pltpu.VMEM((rows, padded), f32),
                pltpu.VMEM((M, rows, padded), f32),
                pltpu.VMEM((M, rows, padded), f32),
                pltpu.VMEM((M, rows, padded), f32),
                pltpu.VMEM((rows, padded), f32),
                pltpu.VMEM((CHUNKS, M, rows, chunk), f32),
                pltpu.VMEM((3, rows, LANE), f32),
                pltpu.VMEM((slices, 8, LANE), f32),
                pltpu.VMEM((M, 8, LANE), f32),
                dma((2, 3)),
                dma((CHUNKS,)), dma((CHUNKS,)), dma((CHUNKS,)),
                dma((CHUNKS,)), dma((CHUNKS,)), dma((CHUNKS,)),
                dma((CHUNKS, M)), dma((CHUNKS, M)), dma((CHUNKS,)),
                dma((slices,)), dma((slices,)), dma((M,)), dma((M,)),
            ],
            compiler_params=pltpu.CompilerParams(
                collective_id=0, has_side_effects=True, vmem_limit_bytes=48 * 1024 * 1024
            ),
        )(slice_starts, coupling)
        return values[None, None], logs[:3, :systems]

    return jax.shard_map(
        body,
        mesh=mesh,
        in_specs=(P("tm", None, None), P()),
        out_specs=(P("tm", "node", None, None), P()),
        check_vma=False,
    )
```

profile of v0, /device:TPU:0, one launch (start us, length us, event | category | flops | bytes accessed | tf_op | source)
XLA Modules:
  0.0 53.0 jit_solution(10155539187022670834)
XLA Ops:
  0.6 0.0 copy-start
  0.6 1.6 %copy-done = f32[1,32,16384]{2,1,0:T(8,128)S(1)} copy-done((f32[1,32,16384]{2,1,0:T(8,128)S(1)}, f32[1,32,16384]{2,1,0:T(8,128)}, u32[]{:S(2)}) %copy-start) | copy-done | bytes 2097176
  2.2 48.8 %shard_map.41 = (f32[32,16384]{1,0:T(8,128)S(1)}, f32[8,128]{1,0:T(8,128)S(1)}) custom-call(f32[1,32,16384]{2,1,0:T(8,128)S(1)} %copy-done, f32[32,16384]{1,0:T(8,128)} %coupling_hbm.1), custom_call_target="tpu_custom_call" | custom-call | tf_op jit(solution)/shard_map/pallas_call | solution.py:441
  51.1 0.6 %slice.3 = f32[3,32]{1,0:T(4,128)} slice(f32[8,128]{1,0:T(8,128)S(1)} %get-tuple-element.5), slice={[0:3], [0:32]} | slice | bytes 768 | tf_op jit(solution)/shard_map/slice | solution.py:473
  51.6 1.3 %copy.5 = f32[1,1,32,16384]{3,2,1,0:T(8,128)} copy(f32[1,1,32,16384]{3,2,1,0:T(8,128)S(1)} %bitcast.1) | data formatting | bytes 4194304
Async XLA Ops:
  0.6 1.6 %copy-start = (f32[1,32,16384]{2,1,0:T(8,128)S(1)}, f32[1,32,16384]{2,1,0:T(8,128)}, u32[]{:S(2)}) copy-start(f32[1,32,16384]{2,1,0:T(8,128)} %start_hbm.1) | copy-start | bytes 6291460
where the time goes:
time: 53.1 us; the launch traced here: 53 us
  Pallas kernels  48.8 us (92%)
  local copies, waits for them, and re-layouts  3.48 us (7%)
  between operations  0.65 us (1%)
    pallas_call x1, Pallas kernels, body(): pl.pallas_call(functools.partial(kernel, slices, rows, cells), out_shape=...  48.8 us
    unnamed x3, local copies, waits for them, and re-layouts  2.9 us

commit v1 on v0

--- a/solution.py
+++ b/solution.py
@@ -353,7 +353,7 @@
 
         over(c, 0, stage_c)
 
-        target = out_hbm.at[my_rows, pl.ds(base_lane, chunk)]
+        target = out_hbm.at[0, 0, my_rows, pl.ds(base_lane, chunk)]
         for step in (2, 3, 1):
             peer = lax.rem(n + step, M)
             remote(result.at[c, peer], target, s_out.at[c, step], r_out.at[c, step], p, peer).start()
@@ -396,7 +396,7 @@
     summed = part_node[0]
     for index in range(1, M):
         summed = summed + part_node[index]
-    log_ref[...] = jnp.log(log_floor + summed / (slices * M * cells))
+    log_ref[...] = jnp.log(log_floor + summed / (slices * M * cells))[:3, :M * rows]
 
     for copy in sends:
         copy.wait_send()
@@ -404,11 +404,11 @@
         here_rows = pl.ds(c * chunk, chunk)
         for step in range(1, M):
             source = lax.rem(n - step + M, M)
-            landed = out_hbm.at[pl.ds(pl.multiple_of(source * rows, rows), rows), here_rows]
+            landed = out_hbm.at[0, 0, pl.ds(pl.multiple_of(source * rows, rows), rows), here_rows]
             arrived = remote(result.at[c, n], landed, s_out.at[c, step], r_out.at[c, step], p, n)
             arrived.wait_recv()
             arrived.wait_send()
-        pltpu.make_async_copy(result.at[c, n], out_hbm.at[my_rows, here_rows], local_sem.at[c]).wait()
+        pltpu.make_async_copy(result.at[c, n], out_hbm.at[0, 0, my_rows, here_rows], local_sem.at[c]).wait()
 
         @pl.when(has_ahead)
         def _():
@@ -437,15 +437,15 @@
         padded = cells + 2 * PAD * LANE
         f32 = jnp.float32
         dma = pltpu.SemaphoreType.DMA
-        anywhere = pl.BlockSpec(memory_space=pl.ANY)
+        anywhere = pl.BlockSpec(memory_space=pltpu.HBM)
         values, logs = pl.pallas_call(
             functools.partial(kernel, slices, rows, cells),
             out_shape=(
-                jax.ShapeDtypeStruct((systems, cells), f32),
-                jax.ShapeDtypeStruct((8, LANE), f32),
+                jax.ShapeDtypeStruct((1, 1, systems, cells), f32),
+                jax.ShapeDtypeStruct((3, systems), f32),
             ),
             in_specs=[anywhere, anywhere],
-            out_specs=(anywhere, pl.BlockSpec(memory_space=pltpu.VMEM)),
+            out_specs=(pl.BlockSpec(memory_space=pl.ANY), pl.BlockSpec(memory_space=pltpu.VMEM)),
             scratch_shapes=[
                 pltpu.VMEM((rows, padded), f32),
                 pltpu.VMEM((rows, padded), f32),
@@ -469,8 +469,11 @@
             compiler_params=pltpu.CompilerParams(
                 collective_id=0, has_side_effects=True, vmem_limit_bytes=48 * 1024 * 1024
             ),
-        )(slice_starts, coupling)
-        return values[None, None], logs[:3, :systems]
+        )(
+            pltpu.with_memory_space_constraint(slice_starts, pltpu.HBM),
+            pltpu.with_memory_space_constraint(coupling, pltpu.HBM),
+        )
+        return values, logs
 
     return jax.shard_map(
         body,

time: 53.1 us -> 51.5 us (0.970)
  local copies, waits for them, and re-layouts: 3.48 us -> 1.9 us
    unnamed x3 -> x2, local copies, waits for them, and re-layouts: 2.9 us -> 1.9 us
    slice x1 -> x0, local copies, waits for them, and re-layouts: 0.58 us -> none  [body(): return (values[None, None], logs[:3, :systems])]
where the time goes in v1:
time: 51.5 us; the launch traced here: 51.3 us
  Pallas kernels  48.8 us (95%)
  local copies, waits for them, and re-layouts  1.9 us (4%)
  between operations  0.64 us (1%)
    pallas_call x1, Pallas kernels, body(): pl.pallas_call(functools.partial(kernel, slices, rows, cells), out_shape=...  48.8 us
    unnamed x2, local copies, waits for them, and re-layouts  1.9 us

profile of v1, /device:TPU:0, one launch (start us, length us, event | category | flops | bytes accessed | tf_op | source)
XLA Modules:
  0.0 51.3 jit_solution(1743794286623630023)
XLA Ops:
  0.6 48.8 %shard_map.41 = (f32[1,1,32,16384]{3,2,1,0:T(8,128)S(1)}, f32[3,32]{1,0:T(4,128)S(1)}) custom-call(f32[1,32,16384]{2,1,0:T(8,128)} %start_hbm.1, f32[32,16384]{1,0:T(8,128)} %coupling_hbm.1), custom_call_target="tpu_custom_call" | custom-call | tf_op jit(solution)/shard_map/pallas_call | solution.py:441
  49.4 1.3 %copy.6 = f32[1,1,32,16384]{3,2,1,0:T(8,128)} copy(f32[1,1,32,16384]{3,2,1,0:T(8,128)S(1)} %get-tuple-element.4) | data formatting | bytes 4194304
  50.7 0.6 %copy.7 = f32[3,32]{1,0:T(4,128)} copy(f32[3,32]{1,0:T(4,128)S(1)} %get-tuple-element.5) | data formatting | bytes 768

commit v2 on v1

--- a/solution.py
+++ b/solution.py
@@ -7,11 +7,14 @@
 from jax.sharding import PartitionSpec as P
 
 M = 4
-CHUNKS = 8
 STEP = 8
+FIRST = (4, 8, 12)
+SLANT = 1
+REST = 16
 LANE = 128
 HALO = 3
 PAD = 4
+PIECES = 4
 MESH = pl.DeviceIdType.MESH
 
 time_step = 0.5
@@ -68,19 +71,30 @@
     return (node_times, matrix)
 
 
+def plan(tiles):
+    bounds = [0]
+    for size in FIRST:
+        bounds.append(bounds[-1] + size)
+    while bounds[-1] < tiles:
+        bounds.append(min(bounds[-1] + REST, tiles))
+    return bounds
+
+
 def kernel(
     slices, rows, cells,
     start_hbm, coupling_hbm, out_hbm, log_ref,
-    own, couple, prev1, prev2, prev3, here, there, mid, before, result,
+    log_tile, log_sem,
+    own, couple, prev1, prev2, prev3, relay, here, there, mid, before, result,
     acc, part_tm, part_node,
     load_sem, s_prev1, r_prev1, s_prev2, r_prev2, s_prev3, r_prev3,
+    s_relay, r_relay, s_side, s_diag, far,
     s_out, r_out, local_sem, s_tm, r_tm, s_node, r_node,
 ):
     p = lax.axis_index("tm")
     n = lax.axis_index("node")
-    chunk = cells // CHUNKS
-    tiles = chunk // LANE
     all_tiles = cells // LANE
+    bounds = plan(all_tiles)
+    chunks = len(bounds) - 1
     my_rows = pl.ds(pl.multiple_of(n * rows, rows), rows)
     node_times, matrix = collocation(M)
     weight = [[time_step * value for value in line] for line in matrix]
@@ -100,23 +114,69 @@
             copy = pltpu.make_async_copy(
                 source.at[:, pl.ds(lo, size)],
                 target.at[:, pl.ds(to, size)],
-                load_sem.at[index, piece],
+                load_sem.at[index],
             )
             copy.start()
-            loads.append(copy)
+        whole = cells + 2 * HALO * LANE
+        loads.append(
+            pltpu.make_async_copy(
+                target.at[:, pl.ds(0, whole)], target.at[:, pl.ds(0, whole)], load_sem.at[index]
+            )
+        )
+
+    partner = jnp.where(even, p + 1, p - 1)
+    ahead = lax.rem(p + 2, slices)
+    behind = lax.rem(p + slices - 2, slices)
+    has_behind = p >= 2
+    has_ahead = p + 2 < slices
+    odd = jnp.logical_not(even)
+    along = has_behind.astype(jnp.int32) + has_ahead.astype(jnp.int32)
+    slanted = jnp.where(even, has_behind, has_ahead)
+    slant = jnp.where(even, lax.rem(p + slices - 1, slices), lax.rem(p + 1, slices))
+
+    def signal(semaphore, tm, node):
+        pl.semaphore_signal(
+            semaphore, inc=1, device_id={"tm": tm, "node": node}, device_id_type=MESH
+        )
+
+    def signal_along(semaphore):
+        @pl.when(has_behind)
+        def _():
+            signal(semaphore, behind, n)
+
+        @pl.when(has_ahead)
+        def _():
+            signal(semaphore, ahead, n)
 
     barrier = pltpu.get_barrier_semaphore()
-    for step in range(1, slices):
-        pl.semaphore_signal(
-            barrier, inc=1, device_id={"tm": lax.rem(p + step, slices), "node": n}, device_id_type=MESH
-        )
+    signal_along(barrier)
+
+    @pl.when(slanted)
+    def _():
+        signal(barrier, slant, n)
+
+    signal(barrier, partner, n)
     for step in range(1, M):
-        pl.semaphore_signal(
-            barrier, inc=1, device_id={"tm": p, "node": lax.rem(n + step, M)}, device_id_type=MESH
-        )
-    pl.semaphore_wait(barrier, slices - 1 + M - 1)
+        signal(barrier, p, lax.rem(n + step, M))
+    pl.semaphore_wait(barrier, along + slanted.astype(jnp.int32) + M)
+    rounds = max(slices // 2 - 2, 0)
+
+    def meet(index):
+        if 0 < index <= rounds:
+            pl.semaphore_wait(far.at[index - 1], along)
+        if index < rounds:
+            signal_along(far.at[index])
+        if index == rounds:
+            signal(far.at[rounds], partner, n)
+        if index == rounds + 1:
+            pl.semaphore_wait(far.at[rounds], 1)
+
+    meet(0)
     for copy in loads:
         copy.wait()
+
+    def shape_of(count):
+        return prev3.at[:, pl.ds(0, count * LANE)]
 
     def remote(source, target, send, recv, tm, node):
         return pltpu.make_async_remote_copy(
@@ -124,39 +184,57 @@
             device_id={"tm": tm, "node": node}, device_id_type=MESH,
         )
 
-    partner = jnp.where(even, p + 1, p - 1)
-    ahead = lax.rem(p + 2, slices)
-
     def part(ref, c):
-        begin = (c * tiles + HALO if c else -HALO) + PAD
-        end = (c + 1) * tiles + HALO + PAD
+        begin = (bounds[c] + HALO if c else -HALO) + PAD
+        end = bounds[c + 1] + HALO + PAD
         return ref.at[:, pl.ds(begin * LANE, (end - begin) * LANE)]
 
     def to_partner_own(c):
-        return remote(part(own, c), part(prev1, c), s_prev1.at[c], r_prev1.at[c], partner, n)
+        return remote(part(own, c), part(prev1, c), s_prev1, r_prev1.at[c], partner, n)
 
     def to_partner_forward(c):
-        return remote(part(prev2, c), part(prev1, c), s_prev1.at[c], r_prev1.at[c], partner, n)
+        return remote(part(prev2, c), part(prev1, c), s_prev1, r_prev1.at[c], partner, n)
+
+    def slant_own(c):
+        return remote(part(own, c), part(prev1, c), s_diag, r_prev1.at[c], slant, n)
 
     def ahead_own(c):
-        return remote(part(own, c), part(prev2, c), s_prev2.at[c], r_prev2.at[c], ahead, n)
+        return remote(part(own, c), part(prev2, c), s_prev2, r_prev2.at[c], ahead, n)
 
     def ahead_forward(c):
-        return remote(part(prev1, c), part(prev3, c), s_prev3.at[c], r_prev3.at[c], ahead, n)
-
-    has_behind = p >= 2
-    has_ahead = p + 2 < slices
-    odd = jnp.logical_not(even)
+        return remote(part(prev1, c), part(prev3, c), s_prev3, r_prev3.at[c], ahead, n)
+
+    def relay_forward(c):
+        return remote(part(prev2, c), part(relay, c), s_relay, r_relay.at[c], ahead, n)
+
+    def to_partner_relayed(c):
+        return remote(part(relay, c), part(prev3, c), s_side, r_prev3.at[c], partner, n)
+
+    def to_partner_second(c):
+        return remote(part(prev2, c), part(prev3, c), s_side, r_prev3.at[c], partner, n)
+
+    def relayed(c):
+        return c % 3 == 2
+
+    def crossed(c):
+        return c % 3 != 1
+
+    def sends_third(c):
+        if relayed(c):
+            return None
+        if crossed(c):
+            return jnp.logical_and(has_ahead, jnp.logical_and(even, has_behind))
+        return jnp.logical_and(has_ahead, jnp.logical_not(first))
 
     def start_ahead(c):
         @pl.when(has_ahead)
         def _():
             ahead_own(c).start()
 
-    @pl.when(even)
-    def _():
-        for c in range(CHUNKS):
+        @pl.when(even)
+        def _():
             to_partner_own(c).start()
+
     def pass_across(c):
         @pl.when(has_behind)
         def _():
@@ -164,7 +242,27 @@
 
         @pl.when(jnp.logical_and(odd, has_behind))
         def _():
-            to_partner_forward(c).start()
+            if c >= SLANT:
+                to_partner_forward(c).start()
+            if relayed(c):
+
+                @pl.when(has_ahead)
+                def _():
+                    relay_forward(c).start()
+
+        if crossed(c):
+
+            @pl.when(jnp.logical_and(even, has_behind))
+            def _():
+                to_partner_second(c).start()
+
+    def pass_back(c):
+        if relayed(c):
+
+            @pl.when(jnp.logical_and(odd, p >= 5))
+            def _():
+                relay_forward(c).wait_recv()
+                to_partner_relayed(c).start()
 
     def pass_ahead(c):
         @pl.when(odd)
@@ -175,11 +273,19 @@
         def _():
             to_partner_forward(c).wait_recv()
 
-        @pl.when(jnp.logical_and(has_ahead, jnp.logical_not(first)))
-        def _():
-            ahead_forward(c).start()
-
-    for c in range(3):
+        if not relayed(c):
+
+            @pl.when(sends_third(c))
+            def _():
+                ahead_forward(c).start()
+
+    for c in range(SLANT):
+
+        @pl.when(jnp.logical_and(odd, has_ahead))
+        def _():
+            slant_own(c).start()
+
+    for c in range(min(3, chunks)):
         start_ahead(c)
 
     acc[...] = jnp.zeros_like(acc)
@@ -221,12 +327,12 @@
             block(begin + count * STEP, end - begin - count * STEP, counted)
 
     def over(c, lag, block):
-        begin = c * tiles + lag if c else 0
-        end = min((c + 1) * tiles + lag, all_tiles)
+        begin = bounds[c] + lag if c else 0
+        end = min(bounds[c + 1] + lag, all_tiles)
         if c == 0 and lag:
             block(-lag, lag, False)
         run(begin, end, block, True)
-        if c == CHUNKS - 1 and lag:
+        if c == chunks - 1 and lag:
             block(all_tiles, lag, False)
 
     def lanes(offset):
@@ -239,15 +345,22 @@
         return pl.ds(lanes(tile + PAD), k * LANE)
 
     pass_across(0)
+    pass_ahead(0)
+    start_ahead(3)
     pass_across(1)
-    pass_ahead(0)
-    for c in range(CHUNKS):
-        base_lane = c * chunk
-
-        if c + 3 < CHUNKS:
-            start_ahead(c + 3)
-        if c + 1 < CHUNKS:
-            pass_ahead(c + 1)
+    pass_ahead(1)
+    start_ahead(4)
+    pass_across(2)
+    start_ahead(5)
+    pass_across(3)
+    for c in range(chunks):
+        base_lane = bounds[c] * LANE
+        chunk = (bounds[c + 1] - bounds[c]) * LANE
+
+        if c + 6 < chunks:
+            start_ahead(c + 6)
+        if c + 2 < chunks:
+            pass_ahead(c + 2)
 
         @pl.when(p >= 3)
         def _():
@@ -293,8 +406,10 @@
             before[:, at] = jnp.where(second, p1, last)
 
         over(c, 2, stage_a)
-        if c + 2 < CHUNKS:
-            pass_across(c + 2)
+        if c + 4 < chunks:
+            pass_across(c + 4)
+        if c + 2 < chunks:
+            pass_back(c + 2)
 
         def update(source, begin, cw, tile, k, which, counted):
             values = []
@@ -347,18 +462,23 @@
         def stage_c(tile, k, counted):
             cw = couple[:, wide(tile, k)]
             outputs = update(mid, before[:, centre(tile, k)], cw, tile, k, 2, counted)
-            at = pl.ds(lanes(tile - c * tiles), k * LANE)
+            at = pl.ds(lanes(tile), k * LANE)
             for m in range(M):
-                result[c, m, :, at] = outputs[m]
+                result[m, :, at] = outputs[m]
 
         over(c, 0, stage_c)
 
-        target = out_hbm.at[0, 0, my_rows, pl.ds(base_lane, chunk)]
+        if c >= 2:
+            meet(c - 1)
+        here_cells = pl.ds(base_lane, chunk)
+        target = out_hbm.at[0, 0, my_rows, here_cells]
         for step in (2, 3, 1):
             peer = lax.rem(n + step, M)
-            remote(result.at[c, peer], target, s_out.at[c, step], r_out.at[c, step], p, peer).start()
-        pltpu.make_async_copy(result.at[c, n], target, local_sem.at[c]).start()
-
+            remote(result.at[peer, :, here_cells], target, s_out, r_out, p, peer).start()
+        pltpu.make_async_copy(result.at[n, :, here_cells], target, local_sem).start()
+
+    for index in range(max(chunks - 1, 1), rounds + 2):
+        meet(index)
     lane = lax.broadcasted_iota(jnp.int32, (rows, LANE), 1)
     sub = lax.broadcasted_iota(jnp.int32, (rows, LANE), 0)
     place = lax.broadcasted_iota(jnp.int32, (8, LANE), 0)
@@ -370,61 +490,103 @@
         )
         tile_value = tile_value + jnp.where(place == which, row, 0.0)
     part_tm[p] = tile_value
-    sends = []
     for step in range(1, slices):
         copy = remote(
-            part_tm.at[p], part_tm.at[p], s_tm.at[step], r_tm.at[step], lax.rem(p + step, slices), n
+            part_tm.at[p], part_tm.at[p], s_tm, r_tm, lax.rem(p + step, slices), n
         )
         copy.start()
-        sends.append(copy)
-    for step in range(1, slices):
-        source = lax.rem(p - step + slices, slices)
-        remote(part_tm.at[source], part_tm.at[source], s_tm.at[step], r_tm.at[step], p, n).wait_recv()
+    others = part_tm.at[pl.ds(0, slices - 1)]
+    gathered = remote(others, others, s_tm, r_tm, partner, n)
+    gathered.wait_recv()
     summed = part_tm[0]
     for index in range(1, slices):
         summed = summed + part_tm[index]
     part_node[n] = summed
     for step in range(1, M):
         copy = remote(
-            part_node.at[n], part_node.at[n], s_node.at[step], r_node.at[step], p, lax.rem(n + step, M)
+            part_node.at[n], part_node.at[n], s_node, r_node, p, lax.rem(n + step, M)
         )
         copy.start()
-        sends.append(copy)
-    for step in range(1, M):
-        source = lax.rem(n - step + M, M)
-        remote(part_node.at[source], part_node.at[source], s_node.at[step], r_node.at[step], p, n).wait_recv()
+    others = part_node.at[pl.ds(0, M - 1)]
+    spread = remote(others, others, s_node, r_node, partner, n)
+    spread.wait_recv()
     summed = part_node[0]
     for index in range(1, M):
         summed = summed + part_node[index]
-    log_ref[...] = jnp.log(log_floor + summed / (slices * M * cells))[:3, :M * rows]
-
-    for copy in sends:
-        copy.wait_send()
-    for c in range(CHUNKS):
-        here_rows = pl.ds(c * chunk, chunk)
-        for step in range(1, M):
-            source = lax.rem(n - step + M, M)
-            landed = out_hbm.at[0, 0, pl.ds(pl.multiple_of(source * rows, rows), rows), here_rows]
-            arrived = remote(result.at[c, n], landed, s_out.at[c, step], r_out.at[c, step], p, n)
-            arrived.wait_recv()
-            arrived.wait_send()
-        pltpu.make_async_copy(result.at[c, n], out_hbm.at[0, 0, my_rows, here_rows], local_sem.at[c]).wait()
-
-        @pl.when(has_ahead)
-        def _():
-            ahead_own(c).wait_send()
-
-        @pl.when(jnp.logical_and(has_ahead, jnp.logical_not(first)))
-        def _():
-            ahead_forward(c).wait_send()
-
-        @pl.when(even)
-        def _():
-            to_partner_own(c).wait_send()
-
-        @pl.when(jnp.logical_and(odd, has_behind))
-        def _():
-            to_partner_forward(c).wait_send()
+    log_tile[...] = jnp.log(log_floor + summed / (slices * M * cells))[:3, :M * rows]
+    log_copy = pltpu.make_async_copy(log_tile, log_ref, log_sem)
+    log_copy.start()
+
+    log_copy.wait()
+    gathered.wait_send()
+    spread.wait_send()
+    three = result.at[pl.ds(0, M - 1)]
+    outputs = remote(three, three, s_out, r_out, partner, n)
+    outputs.wait_send()
+    outputs.wait_recv()
+    mine = result.at[0]
+    pltpu.make_async_copy(mine, mine, local_sem).wait()
+
+    def span(c):
+        return bounds[c + 1] - bounds[c] + (0 if c else 2 * HALO)
+
+    def drain(semaphore, wanted):
+        count = sum(span(c) for c in range(chunks) if wanted(c))
+        if count:
+            remote(shape_of(count), shape_of(count), semaphore, r_prev3.at[0], partner, n).wait_send()
+
+    def direct(c):
+        return not relayed(c)
+
+    def straight(c):
+        return not crossed(c)
+
+    @pl.when(has_ahead)
+    def _():
+        drain(s_prev2, lambda c: True)
+
+    @pl.when(jnp.logical_and(has_ahead, jnp.logical_and(even, has_behind)))
+    def _():
+        drain(s_prev3, direct)
+
+    @pl.when(jnp.logical_and(has_ahead, odd))
+    def _():
+        drain(s_prev3, straight)
+        drain(s_diag, lambda c: c < SLANT)
+
+    @pl.when(even)
+    def _():
+        drain(s_prev1, lambda c: True)
+
+    @pl.when(jnp.logical_and(odd, has_behind))
+    def _():
+        drain(s_prev1, lambda c: c >= SLANT)
+
+    @pl.when(jnp.logical_and(has_ahead, jnp.logical_and(odd, has_behind)))
+    def _():
+        drain(s_relay, relayed)
+
+    @pl.when(jnp.logical_and(odd, p >= 5))
+    def _():
+        drain(s_side, relayed)
+
+    @pl.when(jnp.logical_and(even, has_behind))
+    def _():
+        drain(s_side, crossed)
+
+
+def unload(values, logs, values_hbm, logs_hbm, sem):
+    size = values.shape[2] // PIECES
+    copies = [pltpu.make_async_copy(logs, logs_hbm, sem.at[PIECES])]
+    for piece in range(PIECES):
+        at = pl.ds(piece * size, size)
+        copies.append(
+            pltpu.make_async_copy(values.at[:, :, at], values_hbm.at[:, :, at], sem.at[piece])
+        )
+    for copy in copies:
+        copy.start()
+    for copy in copies:
+        copy.wait()
 
 
 def solution(mesh):
@@ -433,10 +595,12 @@
     def body(slice_starts, coupling):
         systems, cells = coupling.shape
         rows = systems // M
-        chunk = cells // CHUNKS
+        chunks = len(plan(cells // LANE)) - 1
+        far = max(slices // 2 - 2, 0) + 1
         padded = cells + 2 * PAD * LANE
         f32 = jnp.float32
         dma = pltpu.SemaphoreType.DMA
+        anyplace = pl.BlockSpec(memory_space=pl.ANY)
         anywhere = pl.BlockSpec(memory_space=pltpu.HBM)
         values, logs = pl.pallas_call(
             functools.partial(kernel, slices, rows, cells),
@@ -445,8 +609,10 @@
                 jax.ShapeDtypeStruct((3, systems), f32),
             ),
             in_specs=[anywhere, anywhere],
-            out_specs=(pl.BlockSpec(memory_space=pl.ANY), pl.BlockSpec(memory_space=pltpu.VMEM)),
+            out_specs=(anyplace, anyplace),
             scratch_shapes=[
+                pltpu.VMEM((3, systems), f32), dma,
+                pltpu.VMEM((rows, padded), f32),
                 pltpu.VMEM((rows, padded), f32),
                 pltpu.VMEM((rows, padded), f32),
                 pltpu.VMEM((rows, padded), f32),
@@ -456,15 +622,14 @@
                 pltpu.VMEM((M, rows, padded), f32),
                 pltpu.VMEM((M, rows, padded), f32),
                 pltpu.VMEM((rows, padded), f32),
-                pltpu.VMEM((CHUNKS, M, rows, chunk), f32),
+                pltpu.VMEM((M, rows, cells), f32),
                 pltpu.VMEM((3, rows, LANE), f32),
                 pltpu.VMEM((slices, 8, LANE), f32),
                 pltpu.VMEM((M, 8, LANE), f32),
-                dma((2, 3)),
-                dma((CHUNKS,)), dma((CHUNKS,)), dma((CHUNKS,)),
-                dma((CHUNKS,)), dma((CHUNKS,)), dma((CHUNKS,)),
-                dma((CHUNKS, M)), dma((CHUNKS, M)), dma((CHUNKS,)),
-                dma((slices,)), dma((slices,)), dma((M,)), dma((M,)),
+                dma((2,)),
+                dma, dma((chunks,)), dma, dma((chunks,)), dma, dma((chunks,)),
+                dma, dma((chunks,)), dma, dma, pltpu.SemaphoreType.REGULAR((far,)),
+                dma, dma, dma, dma, dma, dma, dma,
             ],
             compiler_params=pltpu.CompilerParams(
                 collective_id=0, has_side_effects=True, vmem_limit_bytes=48 * 1024 * 1024
@@ -473,7 +638,16 @@
             pltpu.with_memory_space_constraint(slice_starts, pltpu.HBM),
             pltpu.with_memory_space_constraint(coupling, pltpu.HBM),
         )
-        return values, logs
+        return tuple(
+            pl.pallas_call(
+                unload,
+                out_shape=(pltpu.HBM(values.shape, f32), pltpu.HBM(logs.shape, f32)),
+                in_specs=[anyplace, anyplace],
+                out_specs=(anywhere, anywhere),
+                scratch_shapes=[dma((PIECES + 1,))],
+                compiler_params=pltpu.CompilerParams(vmem_limit_bytes=1024 * 1024),
+            )(values, logs)
+        )
 
     return jax.shard_map(
         body,

time: 51.5 us -> 46 us (0.89)
  Pallas kernels: 48.8 us -> 45.2 us
  local copies, waits for them, and re-layouts: 1.9 us -> 0 us
    pallas_call x1, Pallas kernels: 48.8 us -> 43.9 us  [body(): pl.pallas_call(functools.partial(kernel, slices, rows, cells), out_shape=...]
    unnamed x2 -> x0, local copies, waits for them, and re-layouts: 1.9 us -> none
    pallas_call x0 -> x1, Pallas kernels: none -> 1.36 us  [body(): pl.pallas_call(unload, out_shape=(pltpu.HBM(values.shape, f32), pltpu.HBM...]
where the time goes in v2:
time: 46 us; the launch traced here: 45.8 us
  Pallas kernels  45.2 us (98%)
  between operations  0.64 us (1%)
    pallas_call x1, Pallas kernels, body(): pl.pallas_call(functools.partial(kernel, slices, rows, cells), out_shape=...  43.9 us
    pallas_call x1, Pallas kernels, body(): pl.pallas_call(unload, out_shape=(pltpu.HBM(values.shape, f32), pltpu.HBM...  1.36 us

profile of v2, /device:TPU:0, one launch (start us, length us, event | category | flops | bytes accessed | tf_op | source)
XLA Modules:
  0.0 45.8 jit_solution(3096545487003489192)
XLA Ops:
  0.6 43.9 %shard_map.41 = (f32[1,1,32,16384]{3,2,1,0:T(8,128)S(1)}, f32[3,32]{1,0:T(4,128)S(1)}) custom-call(f32[1,32,16384]{2,1,0:T(8,128)} %start_hbm.1, f32[32,16384]{1,0:T(8,128)} %coupling_hbm.1), custom_call_target="tpu_custom_call" | custom-call | tf_op jit(solution)/shard_map/pallas_call | solution.py:605
  44.5 1.4 %shard_map.42 = (f32[1,1,32,16384]{3,2,1,0:T(8,128)}, f32[3,32]{1,0:T(4,128)}) custom-call(f32[1,1,32,16384]{3,2,1,0:T(8,128)S(1)} %get-tuple-element.4.values, f32[3,32]{1,0:T(4,128)S(1)} %get-tuple-element.5.logs), custom_call_target="tpu_custom_call" | custom-call | tf_op jit(solution)/shard_map/pallas_call | solution.py:642

commit v3 on v2

--- a/solution.py
+++ b/solution.py
@@ -7,14 +7,18 @@
 from jax.sharding import PartitionSpec as P
 
 M = 4
-STEP = 8
+STEP = 16
 FIRST = (4, 8, 12)
-SLANT = 1
+SLANT = 2
+KINDS = (1, 1, 1, 2, 0, 1, 2, 0, 1, 2, 0)
+START = (("even", 3), ("odd", 4), ("across", 1), ("ahead", 1), ("even", 4), ("across", 2), ("ahead", 2), ("even", 5), ("odd", 5), ("across", 3))
+STEADY = ((0, "odd", 6), (1, "ahead", 3), (1, "even", 6), (2, "across", 5), (2, "back", 3))
+EARLY = {(0, "ahead"): 2, (1, "ahead"): 2, (0, "across"): 4, (1, "across"): 4, (0, "back"): 1, (1, "back"): 2}
 REST = 16
 LANE = 128
 HALO = 3
 PAD = 4
-PIECES = 4
+PIECES = 1
 MESH = pl.DeviceIdType.MESH
 
 time_step = 0.5
@@ -98,7 +102,6 @@
     my_rows = pl.ds(pl.multiple_of(n * rows, rows), rows)
     node_times, matrix = collocation(M)
     weight = [[time_step * value for value in line] for line in matrix]
-    total = [sum(line) for line in weight]
     implicit = [time_step * moment / M for moment in node_times]
     even = lax.rem(p, 2) == 0
     first = p == 0
@@ -214,10 +217,10 @@
         return remote(part(prev2, c), part(prev3, c), s_side, r_prev3.at[c], partner, n)
 
     def relayed(c):
-        return c % 3 == 2
+        return KINDS[c % len(KINDS)] == 0
 
     def crossed(c):
-        return c % 3 != 1
+        return KINDS[c % len(KINDS)] != 2
 
     def sends_third(c):
         if relayed(c):
@@ -226,14 +229,21 @@
             return jnp.logical_and(has_ahead, jnp.logical_and(even, has_behind))
         return jnp.logical_and(has_ahead, jnp.logical_not(first))
 
-    def start_ahead(c):
-        @pl.when(has_ahead)
-        def _():
+    def start_even(c):
+        @pl.when(even)
+        def _():
+            to_partner_own(c).start()
+
+            @pl.when(has_ahead)
+            def _():
+                ahead_own(c).start()
+
+    def start_odd(c):
+        @pl.when(jnp.logical_and(odd, has_ahead))
+        def _():
+            if c < SLANT:
+                slant_own(c).start()
             ahead_own(c).start()
-
-        @pl.when(even)
-        def _():
-            to_partner_own(c).start()
 
     def pass_across(c):
         @pl.when(has_behind)
@@ -278,15 +288,6 @@
             @pl.when(sends_third(c))
             def _():
                 ahead_forward(c).start()
-
-    for c in range(SLANT):
-
-        @pl.when(jnp.logical_and(odd, has_ahead))
-        def _():
-            slant_own(c).start()
-
-    for c in range(min(3, chunks)):
-        start_ahead(c)
 
     acc[...] = jnp.zeros_like(acc)
 
@@ -297,17 +298,32 @@
         left = pltpu.roll(flux, 1, 1)
         return (flux - left)[:, LANE:LANE + k * LANE]
 
-    def two_steps(base, u, square, reaction, a):
-        s = (3.0 * a) * square - a
-        d = 1.0 + s
-        top = base + u * s
-        target = base - a * reaction
+    def finish(d, top, target, a):
         dd = d * d
         tt = top * top
         above = target * (d * dd) + (2.0 * a) * (top * tt)
         below = d * ((1.0 - a) * dd + (3.0 * a) * tt)
         guess = pl.reciprocal(below, approx=True)
         return above * (guess * (2.0 - below * guess))
+
+    def two_steps(base, defect, u, square, reaction, a):
+        d = (3.0 * a) * square + (1.0 - a)
+        return finish(d, defect + u * d, base - a * reaction, a)
+
+    def equal_nodes(begin, vw, cw, k):
+        v = vw[:, LANE:LANE + k * LANE]
+        square = v * v
+        reaction = v - v * square
+        four = 4.0 * (diffusion(vw, cw, k) + reaction)
+        slope = 3.0 * square - 1.0
+        lift = four + v * slope
+        pull = four - reaction
+
+        def node(m):
+            a = implicit[m]
+            return finish(1.0 + a * slope, begin + a * lift, begin + a * pull, a)
+
+        return v, four, node
 
     def folded(value, k):
         out = value[:, :LANE]
@@ -344,72 +360,69 @@
     def centre(tile, k):
         return pl.ds(lanes(tile + PAD), k * LANE)
 
-    pass_across(0)
-    pass_ahead(0)
-    start_ahead(3)
-    pass_across(1)
-    pass_ahead(1)
-    start_ahead(4)
-    pass_across(2)
-    start_ahead(5)
-    pass_across(3)
+    begun = {"even": 0, "odd": 0, "across": 0, "ahead": 0, "back": 0}
+    moves = {
+        "even": start_even, "odd": start_odd,
+        "across": pass_across, "ahead": pass_ahead, "back": pass_back,
+    }
+
+    def proceed(name, upto):
+        for index in range(begun[name], min(upto, chunks)):
+            moves[name](index)
+        begun[name] = max(begun[name], upto)
+
+    for name, upto in START:
+        proceed(name, upto)
+
+    def stage(k, place):
+        for at, name, lead in STEADY:
+            if at == place:
+                slack = EARLY.get((k, name), lead)
+                proceed(name, k + slack)
+
     for c in range(chunks):
         base_lane = bounds[c] * LANE
         chunk = (bounds[c + 1] - bounds[c]) * LANE
 
-        if c + 6 < chunks:
-            start_ahead(c + 6)
-        if c + 2 < chunks:
-            pass_ahead(c + 2)
+        stage(c, 0)
+        for name in moves:
+            proceed(name, c + 1)
 
         @pl.when(p >= 3)
         def _():
             ahead_forward(c).wait_recv()
 
         def stage_a(tile, k, counted):
-            mid_slice = slice(LANE, LANE + k * LANE)
+            middle = slice(LANE, LANE + k * LANE)
             cw = couple[:, wide(tile, k)]
             at = centre(tile, k)
             vw = own[:, wide(tile, k)]
-            v = vw[:, mid_slice]
             p1w = jnp.where(first, vw, prev1[:, wide(tile, k)])
-            p1 = p1w[:, mid_slice]
+            p1 = p1w[:, middle]
             p2w = jnp.where(p <= 1, p1w, prev2[:, wide(tile, k)])
-            p2 = p2w[:, mid_slice]
+            p2 = p2w[:, middle]
             p3 = jnp.where(p <= 2, p2, prev3[:, at])
 
-            square = v * v
-            reaction = v - v * square
-            forcing = diffusion(vw, cw, k) + reaction
-            found = None
+            v, four, node = equal_nodes(p1, vw, cw, k)
             for m in range(M):
-                base = p1 + total[m] * forcing
-                if counted:
-                    defect = base - v
-                    found = defect * defect if found is None else found + defect * defect
-                here[m, :, at] = two_steps(base, v, square, reaction, implicit[m])
+                here[m, :, at] = node(m)
             if counted:
-                acc[0] += folded(found, k)
-
-            square = p1 * p1
-            reaction = p1 - p1 * square
-            forcing = diffusion(p1w, cw, k) + reaction
+                gap = p1 - v
+                cross = 2.0 * sum(implicit)
+                curve = sum(a * a for a in implicit)
+                acc[0] += folded(
+                    gap * (float(M) * gap + cross * four) + curve * (four * four), k
+                )
+
+            _, _, node = equal_nodes(p2, p1w, cw, k)
             for m in range(M):
-                there[m, :, at] = two_steps(p2 + total[m] * forcing, p1, square, reaction, implicit[m])
-
-            square = p2 * p2
-            reaction = p2 - p2 * square
-            forcing = diffusion(p2w, cw, k) + reaction
-            last = two_steps(
-                p3 + total[M - 1] * forcing, p2, square, reaction, implicit[M - 1]
-            )
-            before[:, at] = jnp.where(second, p1, last)
+                there[m, :, at] = node(m)
+
+            _, _, node = equal_nodes(p3, p2w, cw, k)
+            before[:, at] = jnp.where(second, p1, node(M - 1))
 
         over(c, 2, stage_a)
-        if c + 4 < chunks:
-            pass_across(c + 4)
-        if c + 2 < chunks:
-            pass_back(c + 2)
+        stage(c, 1)
 
         def update(source, begin, cw, tile, k, which, counted):
             values = []
@@ -428,10 +441,10 @@
                 for j in range(M):
                     base = base + weight[m][j] * forcings[j]
                 v, square, reaction = values[m]
+                defect = base - v
                 if counted:
-                    defect = base - v
                     found = defect * defect if found is None else found + defect * defect
-                outputs.append(two_steps(base, v, square, reaction, implicit[m]))
+                outputs.append(two_steps(base, defect, v, square, reaction, implicit[m]))
             if counted:
                 acc[which] += folded(found, k)
             return outputs
@@ -454,10 +467,11 @@
                 mixed = w * vw if mixed is None else mixed + w * vw
                 mixed_reaction = w * reaction if mixed_reaction is None else mixed_reaction + w * reaction
             base = before[:, at] + (diffusion(mixed, cw, k) + mixed_reaction)
-            last = two_steps(base, v, square, reaction, implicit[M - 1])
+            last = two_steps(base, base - v, v, square, reaction, implicit[M - 1])
             before[:, at] = jnp.where(first, own[:, centre(tile, k)], last)
 
         over(c, 1, stage_b)
+        stage(c, 2)
 
         def stage_c(tile, k, counted):
             cw = couple[:, wide(tile, k)]

time: 46 us -> 43.6 us (0.948)
  Pallas kernels: 45.2 us -> 42.6 us
    pallas_call x1, Pallas kernels: 43.9 us -> 41.3 us  [body(): pl.pallas_call(functools.partial(kernel, slices, rows, cells), out_shape=...]
where the time goes in v3:
time: 43.6 us; the launch traced here: 43.4 us
  Pallas kernels  42.6 us (98%)
  between operations  0.8 us (2%)
    pallas_call x1, Pallas kernels, body(): pl.pallas_call(functools.partial(kernel, slices, rows, cells), out_shape=...  41.3 us
    pallas_call x1, Pallas kernels, body(): pl.pallas_call(unload, out_shape=(pltpu.HBM(values.shape, f32), pltpu.HBM...  1.34 us

profile of v3, /device:TPU:0, one launch (start us, length us, event | category | flops | bytes accessed | tf_op | source)
XLA Modules:
  0.0 43.4 jit_solution(8653635739872055539)
XLA Ops:
  0.6 41.3 %shard_map.41 = (f32[1,1,32,16384]{3,2,1,0:T(8,128)S(1)}, f32[3,32]{1,0:T(4,128)S(1)}) custom-call(f32[1,32,16384]{2,1,0:T(8,128)} %start_hbm.1, f32[32,16384]{1,0:T(8,128)} %coupling_hbm.1), custom_call_target="tpu_custom_call" | custom-call | tf_op jit(solution)/shard_map/pallas_call | solution.py:619
  41.9 1.3 %shard_map.42 = (f32[1,1,32,16384]{3,2,1,0:T(8,128)}, f32[3,32]{1,0:T(4,128)}) custom-call(f32[1,1,32,16384]{3,2,1,0:T(8,128)S(1)} %get-tuple-element.4.values, f32[3,32]{1,0:T(4,128)S(1)} %get-tuple-element.5.logs), custom_call_target="tpu_custom_call" | custom-call | tf_op jit(solution)/shard_map/pallas_call | solution.py:656

commit v4 on v3

--- a/solution.py
+++ b/solution.py
@@ -12,8 +12,9 @@
 SLANT = 2
 KINDS = (1, 1, 1, 2, 0, 1, 2, 0, 1, 2, 0)
 START = (("even", 3), ("odd", 4), ("across", 1), ("ahead", 1), ("even", 4), ("across", 2), ("ahead", 2), ("even", 5), ("odd", 5), ("across", 3))
-STEADY = ((0, "odd", 6), (1, "ahead", 3), (1, "even", 6), (2, "across", 5), (2, "back", 3))
-EARLY = {(0, "ahead"): 2, (1, "ahead"): 2, (0, "across"): 4, (1, "across"): 4, (0, "back"): 1, (1, "back"): 2}
+STEADY = ((0, "odd", 6), (1, "ahead", 3), (1, "even", 6), (2, "across", 5), (3, "back", 3))
+EARLY = {(0, 0): (("odd", 6),), (0, 1): (("even", 6),), (0, 2): (("across", 4),), (1, 0): (("odd", 7),), (1, 1): (("ahead", 3), ("even", 7)), (1, 2): (("across", 5),), (1, 3): (("ahead", 4), ("back", 3))}
+SETTLED = 2
 REST = 16
 LANE = 128
 HALO = 3
@@ -89,10 +90,10 @@
     start_hbm, coupling_hbm, out_hbm, log_ref,
     log_tile, log_sem,
     own, couple, prev1, prev2, prev3, relay, here, there, mid, before, result,
-    acc, part_tm, part_node,
+    acc, parts,
     load_sem, s_prev1, r_prev1, s_prev2, r_prev2, s_prev3, r_prev3,
     s_relay, r_relay, s_side, s_diag, far,
-    s_out, r_out, local_sem, s_tm, r_tm, s_node, r_node,
+    s_out, r_out, local_sem, s_log, r_log,
 ):
     p = lax.axis_index("tm")
     n = lax.axis_index("node")
@@ -173,6 +174,10 @@
             signal(far.at[rounds], partner, n)
         if index == rounds + 1:
             pl.semaphore_wait(far.at[rounds], 1)
+            for step in range(1, M):
+                signal(far.at[rounds + 1], p, lax.rem(n + step, M))
+        if index == rounds + 2:
+            pl.semaphore_wait(far.at[rounds + 1], M - 1)
 
     meet(0)
     for copy in loads:
@@ -375,10 +380,12 @@
         proceed(name, upto)
 
     def stage(k, place):
-        for at, name, lead in STEADY:
-            if at == place:
-                slack = EARLY.get((k, name), lead)
-                proceed(name, k + slack)
+        for name, upto in EARLY.get((k, place), ()):
+            proceed(name, upto)
+        if k >= SETTLED:
+            for at, name, lead in STEADY:
+                if at == place:
+                    proceed(name, k + lead)
 
     for c in range(chunks):
         base_lane = bounds[c] * LANE
@@ -490,50 +497,38 @@
             peer = lax.rem(n + step, M)
             remote(result.at[peer, :, here_cells], target, s_out, r_out, p, peer).start()
         pltpu.make_async_copy(result.at[n, :, here_cells], target, local_sem).start()
-
-    for index in range(max(chunks - 1, 1), rounds + 2):
+        stage(c, 3)
+
+    for index in range(max(chunks - 1, 1), rounds + 3):
         meet(index)
     lane = lax.broadcasted_iota(jnp.int32, (rows, LANE), 1)
     sub = lax.broadcasted_iota(jnp.int32, (rows, LANE), 0)
-    place = lax.broadcasted_iota(jnp.int32, (8, LANE), 0)
-    tile_value = jnp.zeros((8, LANE), jnp.float32)
+    mixed = jnp.zeros((rows, LANE), jnp.float32)
     for which in range(3):
         per_system = jnp.sum(acc[which], axis=1, keepdims=True)
-        row = jnp.sum(
-            jnp.where(lane == n * rows + sub, per_system, 0.0), axis=0, keepdims=True
-        )
-        tile_value = tile_value + jnp.where(place == which, row, 0.0)
-    part_tm[p] = tile_value
-    for step in range(1, slices):
-        copy = remote(
-            part_tm.at[p], part_tm.at[p], s_tm, r_tm, lax.rem(p + step, slices), n
-        )
-        copy.start()
-    others = part_tm.at[pl.ds(0, slices - 1)]
-    gathered = remote(others, others, s_tm, r_tm, partner, n)
+        place = which * M * rows + n * rows + sub
+        mixed = mixed + jnp.where(lane == place, per_system, 0.0)
+    slot = p * M + n
+    parts[slot] = jnp.sum(mixed, axis=0, keepdims=True)
+    for other in range(slices - 1, -1, -1):
+        for step in range(M - 1, -1, -1):
+            if other or step:
+                remote(
+                    parts.at[slot], parts.at[slot], s_log, r_log,
+                    lax.rem(p + other, slices), lax.rem(n + step, M),
+                ).start()
+    others = parts.at[pl.ds(0, slices * M - 1)]
+    gathered = remote(others, others, s_log, r_log, partner, n)
     gathered.wait_recv()
-    summed = part_tm[0]
-    for index in range(1, slices):
-        summed = summed + part_tm[index]
-    part_node[n] = summed
-    for step in range(1, M):
-        copy = remote(
-            part_node.at[n], part_node.at[n], s_node, r_node, p, lax.rem(n + step, M)
-        )
-        copy.start()
-    others = part_node.at[pl.ds(0, M - 1)]
-    spread = remote(others, others, s_node, r_node, partner, n)
-    spread.wait_recv()
-    summed = part_node[0]
-    for index in range(1, M):
-        summed = summed + part_node[index]
-    log_tile[...] = jnp.log(log_floor + summed / (slices * M * cells))[:3, :M * rows]
+    summed = jnp.sum(parts[...], axis=0)
+    logs = jnp.log(log_floor + summed / (slices * M * cells))
+    for which in range(3):
+        log_tile[which:which + 1, :] = logs[:, which * M * rows:(which + 1) * M * rows]
     log_copy = pltpu.make_async_copy(log_tile, log_ref, log_sem)
     log_copy.start()
 
     log_copy.wait()
     gathered.wait_send()
-    spread.wait_send()
     three = result.at[pl.ds(0, M - 1)]
     outputs = remote(three, three, s_out, r_out, partner, n)
     outputs.wait_send()
@@ -610,7 +605,7 @@
         systems, cells = coupling.shape
         rows = systems // M
         chunks = len(plan(cells // LANE)) - 1
-        far = max(slices // 2 - 2, 0) + 1
+        far = max(slices // 2 - 2, 0) + 2
         padded = cells + 2 * PAD * LANE
         f32 = jnp.float32
         dma = pltpu.SemaphoreType.DMA
@@ -638,12 +633,11 @@
                 pltpu.VMEM((rows, padded), f32),
                 pltpu.VMEM((M, rows, cells), f32),
                 pltpu.VMEM((3, rows, LANE), f32),
-                pltpu.VMEM((slices, 8, LANE), f32),
-                pltpu.VMEM((M, 8, LANE), f32),
+                pltpu.VMEM((slices * M, 1, LANE), f32),
                 dma((2,)),
                 dma, dma((chunks,)), dma, dma((chunks,)), dma, dma((chunks,)),
                 dma, dma((chunks,)), dma, dma, pltpu.SemaphoreType.REGULAR((far,)),
-                dma, dma, dma, dma, dma, dma, dma,
+                dma, dma, dma, dma, dma,
             ],
             compiler_params=pltpu.CompilerParams(
                 collective_id=0, has_side_effects=True, vmem_limit_bytes=48 * 1024 * 1024

time: 43.6 us -> 41.7 us (0.956)
  the two profiles are of different devices: /device:TPU:0 before, /device:TPU:25 now
where the time goes in v4:
time: 41.7 us; the launch traced here: 41.6 us
  Pallas kernels  40.8 us (98%)
  between operations  0.8 us (2%)
    pallas_call x1, Pallas kernels, body(): pl.pallas_call(functools.partial(kernel, slices, rows, cells), out_shape=...  39.5 us
    pallas_call x1, Pallas kernels, body(): pl.pallas_call(unload, out_shape=(pltpu.HBM(values.shape, f32), pltpu.HBM...  1.34 us

profile of v4, /device:TPU:25, one launch (start us, length us, event | category | flops | bytes accessed | tf_op | source)
XLA Modules:
  0.0 41.6 jit_solution(17089688857758400156)
XLA Ops:
  0.6 39.5 %shard_map.41 = (f32[1,1,32,16384]{3,2,1,0:T(8,128)S(1)}, f32[3,32]{1,0:T(4,128)S(1)}) custom-call(f32[1,32,16384]{2,1,0:T(8,128)} %start_hbm.1, f32[32,16384]{1,0:T(8,128)} %coupling_hbm.1), custom_call_target="tpu_custom_call" | custom-call | tf_op jit(solution)/shard_map/pallas_call | solution.py:614
  40.1 1.3 %shard_map.42 = (f32[1,1,32,16384]{3,2,1,0:T(8,128)}, f32[3,32]{1,0:T(4,128)}) custom-call(f32[1,1,32,16384]{3,2,1,0:T(8,128)S(1)} %get-tuple-element.4.values, f32[3,32]{1,0:T(4,128)S(1)} %get-tuple-element.5.logs), custom_call_target="tpu_custom_call" | custom-call | tf_op jit(solution)/shard_map/pallas_call | solution.py:650

commit v5 on v4

--- a/solution.py
+++ b/solution.py
@@ -8,7 +8,7 @@
 
 M = 4
 STEP = 16
-FIRST = (4, 8, 12)
+FIRST = (6, 10, 16)
 SLANT = 2
 KINDS = (1, 1, 1, 2, 0, 1, 2, 0, 1, 2, 0)
 START = (("even", 3), ("odd", 4), ("across", 1), ("ahead", 1), ("even", 4), ("across", 2), ("ahead", 2), ("even", 5), ("odd", 5), ("across", 3))

time: 41.7 us -> 41.4 us (level)
  the two profiles are of different devices: /device:TPU:25 before, /device:TPU:0 now
where the time goes in v5:
time: 41.4 us; the launch traced here: 40.9 us
  Pallas kernels  40.1 us (97%)
  between operations  0.8 us (2%)
    pallas_call x1, Pallas kernels, body(): pl.pallas_call(functools.partial(kernel, slices, rows, cells), out_shape=...  38.8 us
    pallas_call x1, Pallas kernels, body(): pl.pallas_call(unload, out_shape=(pltpu.HBM(values.shape, f32), pltpu.HBM...  1.34 us

profile of v5, /device:TPU:0, one launch (start us, length us, event | category | flops | bytes accessed | tf_op | source)
XLA Modules:
  0.0 40.9 jit_solution(4113419217283915816)
XLA Ops:
  0.6 38.8 %shard_map.41 = (f32[1,1,32,16384]{3,2,1,0:T(8,128)S(1)}, f32[3,32]{1,0:T(4,128)S(1)}) custom-call(f32[1,32,16384]{2,1,0:T(8,128)} %start_hbm.1, f32[32,16384]{1,0:T(8,128)} %coupling_hbm.1), custom_call_target="tpu_custom_call" | custom-call | tf_op jit(solution)/shard_map/pallas_call | solution.py:614
  39.4 1.3 %shard_map.42 = (f32[1,1,32,16384]{3,2,1,0:T(8,128)}, f32[3,32]{1,0:T(4,128)}) custom-call(f32[1,1,32,16384]{3,2,1,0:T(8,128)S(1)} %get-tuple-element.4.values, f32[3,32]{1,0:T(4,128)S(1)} %get-tuple-element.5.logs), custom_call_target="tpu_custom_call" | custom-call | tf_op jit(solution)/shard_map/pallas_call | solution.py:650

commit v6 on v5

--- a/solution.py
+++ b/solution.py
@@ -387,9 +387,15 @@
                 if at == place:
                     proceed(name, k + lead)
 
+    def send_out(c):
+        here_cells = pl.ds(bounds[c] * LANE, (bounds[c + 1] - bounds[c]) * LANE)
+        target = out_hbm.at[0, 0, my_rows, here_cells]
+        for step in (2, 3, 1):
+            peer = lax.rem(n + step, M)
+            remote(result.at[peer, :, here_cells], target, s_out, r_out, p, peer).start()
+        pltpu.make_async_copy(result.at[n, :, here_cells], target, local_sem).start()
+
     for c in range(chunks):
-        base_lane = bounds[c] * LANE
-        chunk = (bounds[c + 1] - bounds[c]) * LANE
 
         stage(c, 0)
         for name in moves:
@@ -491,12 +497,8 @@
 
         if c >= 2:
             meet(c - 1)
-        here_cells = pl.ds(base_lane, chunk)
-        target = out_hbm.at[0, 0, my_rows, here_cells]
-        for step in (2, 3, 1):
-            peer = lax.rem(n + step, M)
-            remote(result.at[peer, :, here_cells], target, s_out, r_out, p, peer).start()
-        pltpu.make_async_copy(result.at[n, :, here_cells], target, local_sem).start()
+        if c + 1 < chunks:
+            send_out(c)
         stage(c, 3)
 
     for index in range(max(chunks - 1, 1), rounds + 3):
@@ -517,6 +519,7 @@
                     parts.at[slot], parts.at[slot], s_log, r_log,
                     lax.rem(p + other, slices), lax.rem(n + step, M),
                 ).start()
+    send_out(chunks - 1)
     others = parts.at[pl.ds(0, slices * M - 1)]
     gathered = remote(others, others, s_log, r_log, partner, n)
     gathered.wait_recv()

time: 41.4 us -> 41.2 us (level)
  no operation moved by 1% of the time
where the time goes in v6:
time: 41.2 us; the launch traced here: 40.7 us
  Pallas kernels  39.9 us (97%)
  between operations  0.8 us (2%)
    pallas_call x1, Pallas kernels, body(): pl.pallas_call(functools.partial(kernel, slices, rows, cells), out_shape=...  38.6 us
    pallas_call x1, Pallas kernels, body(): pl.pallas_call(unload, out_shape=(pltpu.HBM(values.shape, f32), pltpu.HBM...  1.34 us

profile of v6, /device:TPU:0, one launch (start us, length us, event | category | flops | bytes accessed | tf_op | source)
XLA Modules:
  0.0 40.7 jit_solution(17738825477130696913)
XLA Ops:
  0.6 38.6 %shard_map.41 = (f32[1,1,32,16384]{3,2,1,0:T(8,128)S(1)}, f32[3,32]{1,0:T(4,128)S(1)}) custom-call(f32[1,32,16384]{2,1,0:T(8,128)} %start_hbm.1, f32[32,16384]{1,0:T(8,128)} %coupling_hbm.1), custom_call_target="tpu_custom_call" | custom-call | tf_op jit(solution)/shard_map/pallas_call | solution.py:617
  39.2 1.3 %shard_map.42 = (f32[1,1,32,16384]{3,2,1,0:T(8,128)}, f32[3,32]{1,0:T(4,128)}) custom-call(f32[1,1,32,16384]{3,2,1,0:T(8,128)S(1)} %get-tuple-element.4.values, f32[3,32]{1,0:T(4,128)S(1)} %get-tuple-element.5.logs), custom_call_target="tpu_custom_call" | custom-call | tf_op jit(solution)/shard_map/pallas_call | solution.py:653
